TPU v7x, 32 devices: a whole 2x2x4 slice. The times are simulated.
32 devices in a mesh: dp: 8 (over y, x, core), mp: 4 (over z).
Axes of the slice: x: 2, y: 2, z: 4, core: 2. Of those that a mesh axis runs over, the one named last changes fastest.
Arguments:
- layer_in: bfloat16 [16384, 768], P(('dp', 'mp')), may hold values from -6 to 6
- query_proj: bfloat16 [768, 768], P(None, 'mp'), may hold values from -0.21875 to 0.21875
- key_proj: bfloat16 [768, 768], P(None, 'mp'), may hold values from -0.21875 to 0.21875
- value_proj: bfloat16 [768, 768], P(None, 'mp'), may hold values from -0.21875 to 0.21875
- out_proj: bfloat16 [768, 768], P('mp'), may hold values from -1.75 to 1.75
- gate_proj: bfloat16 [768, 2048], P(None, 'mp'), may hold values from -0.21875 to 0.21875
- up_proj: bfloat16 [768, 2048], P(None, 'mp'), may hold values from -0.21875 to 0.21875
- down_proj: bfloat16 [2048, 768], P('mp'), may hold values from -0.125 to 0.125
- first_gain: float32 [768], replicated, may hold values from 0.1 to 1.9
- second_gain: float32 [768], replicated, may hold values from 0.1 to 1.9
- seq_lengths: int32 [16], P('dp'), may hold values from 64 to 1024, as said below
- cotangent: bfloat16 [16384, 768], P(('dp', 'mp')), may hold values from -6 to 6
Outputs:
- layer_out: bfloat16 [16384, 768], P(('dp', 'mp'))
- input_grad: bfloat16 [16384, 768], P(('dp', 'mp'))
- query_grad: float32 [768, 768], P(None, 'mp')
- key_grad: float32 [768, 768], P(None, 'mp')
- value_grad: float32 [768, 768], P(None, 'mp')
- output_grad: float32 [768, 768], P('mp')
- gate_grad: float32 [768, 2048], P(None, 'mp')
- up_grad: float32 [768, 2048], P(None, 'mp')
- down_grad: float32 [2048, 768], P('mp')
- first_grad: float32 [768], replicated
- second_grad: float32 [768], replicated
Inputs may be any that keep to these rules, and one draw needn't show every extreme that they name: Slot i holds a sequence of seq_lengths[i] tokens at its start, the rest of its 1024 rows is padding. Some slot is full in every draw.
All inputs are finite; a program needn't handle non-finite values.
Results may differ from a plain program's by a relative error of at most 0.02.
Values may be sent and summed in bfloat16 or wider, within the bound.
A program may use at most 192 MiB of HBM per device.

v0:
```python
import jax
import jax.numpy as jnp
from jax import lax
from jax.sharding import PartitionSpec as P

HS = 64
SLOT_LEN = 1024


def rms_norm(resid, gain):
    return resid * lax.rsqrt(jnp.mean(resid * resid, axis=-1, keepdims=True) + 1e-05) * gain


def swiglu(gate_pre, up_pre):
    return jax.nn.silu(gate_pre) * up_pre


def rotary_tables(group_rows):
    half = HS // 2
    positions = (jnp.arange(group_rows, dtype=jnp.int32) % SLOT_LEN).astype(jnp.float32)
    freqs = 10000.0 ** (-jnp.arange(half, dtype=jnp.float32) * 2.0 / HS)
    angles = positions[:, None] * freqs[None, :]
    return (jnp.cos(angles)[:, None, :], jnp.sin(angles)[:, None, :])


def rotate(field, cosines, sines):
    half = HS // 2
    first = field[..., :half]
    second = field[..., half:]
    return jnp.concatenate(
        [first * cosines - second * sines, second * cosines + first * sines], axis=-1
    )


def unrotate(grads, cosines, sines):
    half = HS // 2
    first = grads[..., :half]
    second = grads[..., half:]
    return jnp.concatenate(
        [first * cosines + second * sines, second * cosines - first * sines], axis=-1
    )


def cross(left, right):
    return lax.dot_general(
        left, right, (((0,), (0,)), ((), ())), preferred_element_type=jnp.float32
    )


def against(left, right):
    return lax.dot_general(
        left, right, (((1,), (1,)), ((), ())), preferred_element_type=jnp.float32
    )


def block_masks(block_index, block_rows, key_span, valid_len):
    query_pos = block_index * block_rows + jnp.arange(block_rows, dtype=jnp.int32)
    key_pos = jnp.arange(key_span, dtype=jnp.int32)
    allowed = (key_pos[None, :] <= query_pos[:, None]) & (key_pos[None, :] < valid_len)
    present = query_pos < valid_len
    return (allowed, present)


def block_scores(query_block, key_block, allowed):
    scores = (
        jnp.einsum("qhd,khd->hqk", query_block, key_block, preferred_element_type=jnp.float32)
        * 0.125
    )
    return jnp.where(allowed[None], scores, -1e30)


def attend(rot_queries, rot_keys, values_low, seq_lengths):
    block_rows = min(512, SLOT_LEN)
    block_count = SLOT_LEN // block_rows
    mixed_parts = []
    log_norms = []
    for slot_index in range(seq_lengths.shape[0]):
        valid_len = seq_lengths[slot_index]
        base = slot_index * SLOT_LEN
        for block_index in range(block_count):
            start = base + block_index * block_rows
            key_span = (block_index + 1) * block_rows
            allowed, present = block_masks(block_index, block_rows, key_span, valid_len)
            scores = block_scores(
                rot_queries[start : start + block_rows], rot_keys[base : base + key_span], allowed
            )
            top = jnp.max(scores, axis=-1, keepdims=True)
            log_norm = top + jnp.log(jnp.sum(jnp.exp(scores - top), axis=-1, keepdims=True))
            probs_low = jnp.exp(scores - log_norm).astype(jnp.bfloat16)
            mixed = jnp.einsum(
                "hqk,khd->qhd",
                probs_low,
                values_low[base : base + key_span],
                preferred_element_type=jnp.float32,
            )
            mixed_parts.append(mixed * present.astype(jnp.float32)[:, None, None])
            log_norms.append(log_norm)
    return (jnp.concatenate(mixed_parts, axis=0), log_norms)


def attend_back(rot_queries, rot_keys, values_low, d_mixed, log_norms, seq_lengths):
    block_rows = min(512, SLOT_LEN)
    block_count = SLOT_LEN // block_rows
    query_parts = []
    key_parts = []
    value_parts = []
    shape = (SLOT_LEN,) + rot_keys.shape[1:]
    for slot_index in range(seq_lengths.shape[0]):
        valid_len = seq_lengths[slot_index]
        base = slot_index * SLOT_LEN
        key_total = jnp.zeros(shape, jnp.float32)
        value_total = jnp.zeros(shape, jnp.float32)
        for block_index in range(block_count):
            start = base + block_index * block_rows
            key_span = (block_index + 1) * block_rows
            allowed, present = block_masks(block_index, block_rows, key_span, valid_len)
            query_block = rot_queries[start : start + block_rows]
            key_block = rot_keys[base : base + key_span]
            value_block = values_low[base : base + key_span]
            grad_block = (
                d_mixed[start : start + block_rows] * present.astype(jnp.bfloat16)[:, None, None]
            )
            scores = block_scores(query_block, key_block, allowed)
            attn_probs = jnp.exp(scores - log_norms[slot_index * block_count + block_index])
            d_probs = jnp.einsum(
                "qhd,khd->hqk", grad_block, value_block, preferred_element_type=jnp.float32
            )
            d_scores = (
                attn_probs * (d_probs - jnp.sum(d_probs * attn_probs, axis=-1, keepdims=True))
            ).astype(jnp.bfloat16)
            query_parts.append(
                jnp.einsum("hqk,khd->qhd", d_scores, key_block, preferred_element_type=jnp.float32)
                * 0.125
            )
            key_step = (
                jnp.einsum(
                    "hqk,qhd->khd", d_scores, query_block, preferred_element_type=jnp.float32
                )
                * 0.125
            )
            value_step = jnp.einsum(
                "hqk,qhd->khd",
                attn_probs.astype(jnp.bfloat16),
                grad_block,
                preferred_element_type=jnp.float32,
            )
            key_total = key_total.at[:key_span].add(key_step)
            value_total = value_total.at[:key_span].add(value_step)
        key_parts.append(key_total)
        value_parts.append(value_total)
    return (
        jnp.concatenate(query_parts, axis=0),
        jnp.concatenate(key_parts, axis=0),
        jnp.concatenate(value_parts, axis=0),
    )


def body(
    layer_in,
    query_proj,
    key_proj,
    value_proj,
    out_proj,
    gate_proj,
    up_proj,
    down_proj,
    first_gain,
    second_gain,
    seq_lengths,
    cotangent,
):
    head_width = query_proj.shape[1]
    local_heads = head_width // HS
    gathered = lax.all_gather(layer_in, "mp", axis=0, tiled=True)
    group_rows = gathered.shape[0]
    cosines, sines = rotary_tables(group_rows)

    def split_heads(field):
        return field.reshape(group_rows, local_heads, HS)

    rot_queries = rotate(
        split_heads(jnp.dot(gathered, query_proj, preferred_element_type=jnp.float32)),
        cosines,
        sines,
    ).astype(jnp.bfloat16)
    rot_keys = rotate(
        split_heads(jnp.dot(gathered, key_proj, preferred_element_type=jnp.float32)), cosines, sines
    ).astype(jnp.bfloat16)
    values_low = split_heads(
        jnp.dot(gathered, value_proj, preferred_element_type=jnp.float32)
    ).astype(jnp.bfloat16)
    mixed, log_norms = attend(rot_queries, rot_keys, values_low, seq_lengths)
    mixed_low = mixed.reshape(group_rows, head_width).astype(jnp.bfloat16)
    attn_branch = lax.psum_scatter(
        jnp.dot(mixed_low, out_proj, preferred_element_type=jnp.float32).astype(jnp.bfloat16),
        "mp",
        scatter_dimension=0,
        tiled=True,
    ).astype(jnp.float32)
    resid_one = layer_in.astype(jnp.float32) + attn_branch
    normed, first_pull = jax.vjp(rms_norm, resid_one, first_gain)
    normed_all = lax.all_gather(normed.astype(jnp.bfloat16), "mp", axis=0, tiled=True)
    gate_pre = jnp.dot(normed_all, gate_proj, preferred_element_type=jnp.float32)
    up_pre = jnp.dot(normed_all, up_proj, preferred_element_type=jnp.float32)
    hidden = swiglu(gate_pre, up_pre).astype(jnp.bfloat16)
    ffn_branch = lax.psum_scatter(
        jnp.dot(hidden, down_proj, preferred_element_type=jnp.float32).astype(jnp.bfloat16),
        "mp",
        scatter_dimension=0,
        tiled=True,
    ).astype(jnp.float32)
    resid_two = normed + ffn_branch
    result, second_pull = jax.vjp(rms_norm, resid_two, second_gain)
    layer_out = result.astype(jnp.bfloat16)
    d_resid_two, second_part = second_pull(cotangent.astype(jnp.float32))
    ffn_out_all = lax.all_gather(d_resid_two.astype(jnp.bfloat16), "mp", axis=0, tiled=True)
    down_grad = cross(hidden, ffn_out_all)
    d_hidden = against(ffn_out_all, down_proj)
    unused, glu_pull = jax.vjp(swiglu, gate_pre, up_pre)
    d_gate_f, d_up_f = glu_pull(d_hidden)
    d_gate = d_gate_f.astype(jnp.bfloat16)
    d_up = d_up_f.astype(jnp.bfloat16)
    gate_grad = cross(normed_all, d_gate)
    up_grad = cross(normed_all, d_up)
    d_normed = d_resid_two + lax.psum_scatter(
        (against(d_gate, gate_proj) + against(d_up, up_proj)).astype(jnp.bfloat16),
        "mp",
        scatter_dimension=0,
        tiled=True,
    ).astype(jnp.float32)
    d_resid_one, first_part = first_pull(d_normed)
    attn_out_all = lax.all_gather(d_resid_one.astype(jnp.bfloat16), "mp", axis=0, tiled=True)
    output_grad = cross(mixed_low, attn_out_all)
    d_mixed = split_heads(against(attn_out_all, out_proj).astype(jnp.bfloat16))
    d_rot_query, d_rot_key, d_value_raw = attend_back(
        rot_queries, rot_keys, values_low, d_mixed, log_norms, seq_lengths
    )
    d_query = (
        unrotate(d_rot_query, cosines, sines).reshape(group_rows, head_width).astype(jnp.bfloat16)
    )
    d_key = unrotate(d_rot_key, cosines, sines).reshape(group_rows, head_width).astype(jnp.bfloat16)
    d_value = d_value_raw.reshape(group_rows, head_width).astype(jnp.bfloat16)
    query_grad = cross(gathered, d_query)
    key_grad = cross(gathered, d_key)
    value_grad = cross(gathered, d_value)
    input_grad = (
        d_resid_one
        + lax.psum_scatter(
            (
                against(d_query, query_proj)
                + against(d_key, key_proj)
                + against(d_value, value_proj)
            ).astype(jnp.bfloat16),
            "mp",
            scatter_dimension=0,
            tiled=True,
        ).astype(jnp.float32)
    ).astype(jnp.bfloat16)
    query_grad, key_grad, value_grad, output_grad, gate_grad, up_grad, down_grad = lax.psum(
        (query_grad, key_grad, value_grad, output_grad, gate_grad, up_grad, down_grad), "dp"
    )
    first_grad, second_grad = lax.psum((first_part, second_part), ("dp", "mp"))
    return (
        layer_out,
        input_grad,
        query_grad,
        key_grad,
        value_grad,
        output_grad,
        gate_grad,
        up_grad,
        down_grad,
        first_grad,
        second_grad,
    )


def solution(mesh):
    return jax.shard_map(
        body,
        mesh=mesh,
        in_specs=(
            P(("dp", "mp"), None),
            P(None, "mp"),
            P(None, "mp"),
            P(None, "mp"),
            P("mp", None),
            P(None, "mp"),
            P(None, "mp"),
            P("mp", None),
            P(),
            P(),
            P("dp"),
            P(("dp", "mp"), None),
        ),
        out_specs=(
            P(("dp", "mp"), None),
            P(("dp", "mp"), None),
            P(None, "mp"),
            P(None, "mp"),
            P(None, "mp"),
            P("mp", None),
            P(None, "mp"),
            P(None, "mp"),
            P("mp", None),
            P(),
            P(),
        ),
        check_vma=False,
    )
```

profile of v0, /device:TPU:0, one launch (start us, length us, event | category | flops | bytes accessed | tf_op | source)
XLA Modules:
  0.0 745.8 jit_solution(7970744030019012255)
XLA Ops:
  18.3 1.4 fusion.11
  19.7 1.8 multiply_cosine_fusion
  21.5 54.3 %all-gather.5.cloned.1.call-done = bf16[2048,768]{1,0:T(8,128)(2,1)} async-done(((bf16[512,768]{1,0:T(8,128)(2,1)}), bf16[2048,768]{1,0:T(8,128)(2,1)}) %all-gather.5.cloned.1.call-update) | async-done | bytes 3145744 | tf_op jit(solution)/shard_map/all_gather | solution.py:174
  75.8 3.2 convolution_convert_fusion.3
  88.0 3.7 exponential_reduce_fusion
  93.9 2.0 fusion.38
  95.9 2.0 fusion.36
  98.9 2.7 convolution_convert_fusion.1
  101.7 59.1 %reduce-scatter.5.cloned.1.call-done = bf16[512,768]{1,0:T(8,128)(2,1)} async-done(((bf16[2048,768]{1,0:T(8,128)(2,1)}), bf16[512,768]{1,0:T(8,128)(2,1)}) %reduce-scatter.5.cloned.1.call-update) | async-done | bytes 786448 | tf_op jit(solution)/shard_map/reduce_scatter | solution.py:194
  160.9 1.5 multiply_reduce_fusion.7
  162.9 2.3 multiply_convert_fusion.7
  165.3 63.5 %all-gather.7.cloned.1.call-done = bf16[2048,768]{1,0:T(8,128)(2,1)} async-done(((bf16[512,768]{1,0:T(8,128)(2,1)}), bf16[2048,768]{1,0:T(8,128)(2,1)}) %all-gather.7.cloned.1.call-update) | async-done | bytes 3145744 | tf_op jit(solution)/shard_map/all_gather | solution.py:202
  228.8 3.8 fusion.119
  232.7 4.3 multiply_convert_fusion.3
  238.3 3.4 convolution_convert_fusion
  242.2 58.8 %reduce-scatter.7.cloned.1.call-done = bf16[512,768]{1,0:T(8,128)(2,1)} async-done(((bf16[2048,768]{1,0:T(8,128)(2,1)}), bf16[512,768]{1,0:T(8,128)(2,1)}) %reduce-scatter.7.cloned.1.call-update) | async-done | bytes 786448 | tf_op jit(solution)/shard_map/reduce_scatter | solution.py:206
  301.0 1.8 multiply_reduce_fusion.6
  304.0 2.2 fusion.112
  306.3 63.5 %all-gather.9.cloned.1.call-done = bf16[2048,768]{1,0:T(8,128)(2,1)} async-done(((bf16[512,768]{1,0:T(8,128)(2,1)}), bf16[2048,768]{1,0:T(8,128)(2,1)}) %all-gather.9.cloned.1.call-update) | async-done | bytes 3145744 | tf_op jit(solution)/shard_map/all_gather | solution.py:216
  369.7 6.3 multiply_convert_fusion.2
  376.0 1.8 fusion.120
  377.9 3.5 add_convert_fusion.1
  381.5 59.2 %reduce-scatter.9.cloned.1.call-done = bf16[512,768]{1,0:T(8,128)(2,1)} async-done(((bf16[2048,768]{1,0:T(8,128)(2,1)}), bf16[512,768]{1,0:T(8,128)(2,1)}) %reduce-scatter.9.cloned.1.call-update) | async-done | bytes 786448 | tf_op jit(solution)/shard_map/reduce_scatter | solution.py:225
  440.7 3.0 multiply_reduce_fusion.4
  445.0 1.5 fusion.111
  446.7 63.2 %all-gather.11.cloned.1.call-done = bf16[2048,768]{1,0:T(8,128)(2,1)} async-done(((bf16[512,768]{1,0:T(8,128)(2,1)}), bf16[2048,768]{1,0:T(8,128)(2,1)}) %all-gather.11.cloned.1.call-update) | async-done | bytes 3145744 | tf_op jit(solution)/shard_map/all_gather | solution.py:232
  510.0 3.1 convolution_convert_fusion.2
  513.2 3.0 convolution_bitcast_fusion.5
  524.7 2.5 multiply_reduce_fusion.1
  527.3 2.6 fusion.25
  529.9 2.7 multiply_reduce_fusion
  532.6 2.6 fusion.24
  535.2 1.8 multiply_convert_fusion
  538.8 1.8 multiply_convert_fusion.1
  547.9 2.9 add_convert_fusion
  551.1 5.7 fusion.126
  556.8 3.0 fusion.125
  559.8 3.0 fusion.124
  562.7 1.6 fusion.123
  565.1 1.6 convolution_bitcast_fusion.2
  566.7 1.6 convolution_bitcast_fusion.3
  568.3 1.6 convolution_bitcast_fusion.4
  570.6 43.9 %all-reduce.4 = (f32[768]{0:T(1024)}, f32[768]{0:T(1024)}) all-reduce(f32[768]{0:T(1024)S(1)} %copy-done.80, f32[768]{0:T(1024)S(1)} %copy-done.79), channel_id=1, replica_groups=mesh['dp'=8,'mp'=4] {'dp','mp'}, use_global_device_ids=true, to_apply=%region_28.29 | all-reduce | flops 1536 | bytes 12288 | tf_op jit(solution)/shard_map/psum | solution.py:262
  614.5 3.2 add_convert_fusion.2
  617.7 110.9 %all-reduce.8.cloned.1.call-done = (f32[768,192]{0,1:T(8,128)}, f32[768,192]{0,1:T(8,128)}, f32[768,192]{0,1:T(8,128)}, f32[192,768]{1,0:T(8,128)}, f32[768,512]...) async-done(((f32[768,192]{0,1:T(8,128)}, f32[768,192]{0,1:T(8,128)}, f32[768,192]{0,1:T(8,128)}, f32[192,768]{1,0:T(8,128)}, f32[768,512]{1,0:T(8,128)}, ...) | async-done | bytes 7077904 | tf_op jit(solution)/shard_map/psum | solution.py:259
  728.6 2.1 copy.46
  730.6 2.0 copy.47
  732.7 1.9 copy.48
  (276 shorter events, 51.6 us)
Async XLA Ops:
  7.2 231.1 %copy-start = (bf16[512,768]{1,0:T(8,128)(2,1)S(1)}, bf16[512,768]{1,0:T(8,128)(2,1)}, u32[]{:S(2)}) copy-start(bf16[512,768]{1,0:T(8,128)(2,1)} %param.43) | copy-start | bytes 2359300
  7.2 68.6 %all-gather.5.cloned.1.call-start = ((), (), s32[]{:S(2)}) async-start(), calls=%async_computation.4 | async-start | bytes 3932160 | tf_op jit(solution)/shard_map/all_gather | solution.py:174
  7.9 152.9 %reduce-scatter.5.cloned.1.call-start = ((), (), s32[]{:S(2)}) async-start(), calls=%async_computation.5 | async-start | bytes 3932160 | tf_op jit(solution)/shard_map/reduce_scatter | solution.py:194
  18.2 74.7 %copy-start.35 = (pred[512,512]{0,1:T(8,128)(4,1)}, pred[512,512]{0,1:T(8,128)(4,1)S(1)}, u32[]{:S(2)}) copy-start(pred[512,512]{0,1:T(8,128)(4,1)S(1)} %fusion.40) | copy-start | bytes 786436
  18.3 73.4 %copy-start.33 = (pred[512,512]{0,1:T(8,128)(4,1)}, pred[512,512]{0,1:T(8,128)(4,1)S(1)}, u32[]{:S(2)}) copy-start(pred[512,512]{0,1:T(8,128)(4,1)S(1)} %fusion.41) | copy-start | bytes 786436
  19.7 76.2 %copy-start.15 = (pred[512,1024]{1,0:T(8,128)(4,1)}, pred[512,1024]{1,0:T(8,128)(4,1)S(1)}, u32[]{:S(2)}) copy-start(pred[512,1024]{1,0:T(8,128)(4,1)S(1)} %get-tuple-element.182) | copy-start | bytes 1572868
  21.5 57.6 %copy-start.54 = (bf16[768,192]{0,1:T(8,128)(2,1)S(1)}, bf16[768,192]{0,1:T(8,128)(2,1)}, u32[]{:S(2)}) copy-start(bf16[768,192]{0,1:T(8,128)(2,1)} %param.38) | copy-start | bytes 884740
  79.0 12.7 %copy-start.56 = (bf16[512,192]{0,1:T(8,128)(2,1)}, bf16[512,192]{0,1:T(8,128)(2,1)S(1)}, u32[]{:S(2)}) copy-start(bf16[512,192]{0,1:T(8,128)(2,1)S(1)} %get-tuple-element.171) | copy-start | bytes 589828
  79.0 13.8 %copy-start.58 = (bf16[512,192]{0,1:T(8,128)(2,1)}, bf16[512,192]{0,1:T(8,128)(2,1)S(1)}, u32[]{:S(2)}) copy-start(bf16[512,192]{0,1:T(8,128)(2,1)S(1)} %get-tuple-element.172) | copy-start | bytes 589828
  79.1 14.7 %copy-start.47 = (bf16[1024,192]{0,1:T(8,128)(2,1)}, bf16[1024,192]{0,1:T(8,128)(2,1)S(1)}, u32[]{:S(2)}) copy-start(bf16[1024,192]{0,1:T(8,128)(2,1)S(1)} %get-tuple-element.173) | copy-start | bytes 1179652
  79.1 16.7 %copy-start.45 = (bf16[1024,192]{0,1:T(8,128)(2,1)}, bf16[1024,192]{0,1:T(8,128)(2,1)S(1)}, u32[]{:S(2)}) copy-start(bf16[1024,192]{0,1:T(8,128)(2,1)S(1)} %get-tuple-element.174) | copy-start | bytes 1179652
  82.1 4.5 copy-start.43
  82.9 8.9 %copy-start.6 = (f32[3,512,512]{1,2,0:T(8,128)}, f32[3,512,512]{1,2,0:T(8,128)S(1)}, u32[]{:S(2)}) copy-start(f32[3,512,512]{1,2,0:T(8,128)S(1)} %get-tuple-element.192) | copy-start | bytes 9437188
  83.6 8.2 %copy-start.72 = (f32[3,512]{1,0:T(4,128)}, f32[3,512]{1,0:T(4,128)S(1)}, u32[]{:S(2)}) copy-start(f32[3,512]{1,0:T(4,128)S(1)} %log_add_fusion.3) | copy-start | bytes 18436
  84.4 8.4 %copy-start.8 = (f32[3,512,512]{1,2,0:T(8,128)}, f32[3,512,512]{1,2,0:T(8,128)S(1)}, u32[]{:S(2)}) copy-start(f32[3,512,512]{1,2,0:T(8,128)S(1)} %get-tuple-element.188) | copy-start | bytes 9437188
  85.2 7.7 %copy-start.74 = (f32[3,512]{1,0:T(4,128)}, f32[3,512]{1,0:T(4,128)S(1)}, u32[]{:S(2)}) copy-start(f32[3,512]{1,0:T(4,128)S(1)} %log_add_fusion.1) | copy-start | bytes 18436
  86.6 7.3 copy-start.5
  88.0 7.9 %copy-start.4 = (f32[3,512,1024]{2,1,0:T(8,128)}, f32[3,512,1024]{2,1,0:T(8,128)S(1)}, u32[]{:S(2)}) copy-start(f32[3,512,1024]{2,1,0:T(8,128)S(1)} %get-tuple-element.186) | copy-start | bytes 18874372
  91.7 4.2 copy-start.70
  101.6 59.2 %copy-start.10 = (bf16[512,768]{1,0:T(8,128)(2,1)S(1)}, bf16[512,768]{1,0:T(8,128)(2,1)}, u32[]{:S(2)}) copy-start(bf16[512,768]{1,0:T(8,128)(2,1)} %param.36) | copy-start | bytes 2359300
  101.6 61.3 %copy-start.69 = (f32[768]{0:T(1024)S(1)}, f32[768]{0:T(1024)}, u32[]{:S(2)}) copy-start(f32[768]{0:T(1024)} %param.44) | copy-start | bytes 9220
  101.7 127.1 %copy-start.60 = (bf16[768,512]{1,0:T(8,128)(2,1)S(1)}, bf16[768,512]{1,0:T(8,128)(2,1)}, u32[]{:S(2)}) copy-start(bf16[768,512]{1,0:T(8,128)(2,1)} %param.41) | copy-start | bytes 2359300
  101.7 127.1 %all-gather.7.cloned.1.call-start = ((), (), s32[]{:S(2)}) async-start(), calls=%async_computation.6 | async-start | bytes 3932160 | tf_op jit(solution)/shard_map/all_gather | solution.py:202
  165.3 135.7 %reduce-scatter.7.cloned.1.call-start = ((), (), s32[]{:S(2)}) async-start(), calls=%async_computation.7 | async-start | bytes 3932160 | tf_op jit(solution)/shard_map/reduce_scatter | solution.py:206
  228.8 3.9 copy-start.17
  228.8 3.9 copy-start.62
  232.7 4.4 copy-start.90
  241.7 59.2 %copy-start.11 = (bf16[512,768]{1,0:T(8,128)(2,1)S(1)}, bf16[512,768]{1,0:T(8,128)(2,1)}, u32[]{:S(2)}) copy-start(bf16[512,768]{1,0:T(8,128)(2,1)} %reduce-scatter.5.cloned.1.call-done) | copy-start | bytes 2359300
  241.8 127.9 %all-gather.9.cloned.1.call-start = ((), (), s32[]{:S(2)}) async-start(), calls=%async_computation.8 | async-start | bytes 3932160 | tf_op jit(solution)/shard_map/all_gather | solution.py:216
  306.2 134.5 %reduce-scatter.9.cloned.1.call-start = ((), (), s32[]{:S(2)}) async-start(), calls=%async_computation.9 | async-start | bytes 3932160 | tf_op jit(solution)/shard_map/reduce_scatter | solution.py:225
  369.7 6.3 copy-start.61
  381.5 128.5 %all-gather.11.cloned.1.call-start = ((), (), s32[]{:S(2)}) async-start(), calls=%async_computation.10 | async-start | bytes 3932160 | tf_op jit(solution)/shard_map/all_gather | solution.py:232
  440.7 4.3 copy-start.12
  440.7 4.3 copy-start.31
  446.5 66.7 %copy-start.36 = (pred[512,512]{0,1:T(8,128)(4,1)S(1)}, pred[512,512]{0,1:T(8,128)(4,1)}, u32[]{:S(2)}) copy-start(pred[512,512]{0,1:T(8,128)(4,1)} %copy-done.35) | copy-start | bytes 786436
  446.5 66.7 %copy-start.75 = (f32[3,512]{1,0:T(4,128)S(1)}, f32[3,512]{1,0:T(4,128)}, u32[]{:S(2)}) copy-start(f32[3,512]{1,0:T(4,128)} %copy-done.74) | copy-start | bytes 18436
  446.5 66.7 %copy-start.83 = (bf16[512]{0:T(512)(128)(2,1)S(1)}, bf16[512]{0:T(512)(128)(2,1)}, u32[]{:S(2)}) copy-start(bf16[512]{0:T(512)(128)(2,1)} %get-tuple-element.206) | copy-start | bytes 3076
  446.5 168.0 %reduce-scatter.11.cloned.1.call-start = ((), (), s32[]{:S(2)}) async-start(), calls=%async_computation.11 | async-start | bytes 3932160 | tf_op jit(solution)/shard_map/reduce_scatter | solution.py:248
  524.0 5.8 slice-start
  524.7 5.2 slice-start.1
  550.8 177.8 %all-reduce.8.cloned.1.call-start = ((), (), s32[]{:S(2)}) async-start(), calls=%async_computation.12 | async-start | bytes 14155776 | tf_op jit(solution)/shard_map/psum | solution.py:259
  551.1 5.7 copy-start.18
  551.1 5.7 copy-start.26
  569.9 44.6 %copy-start.32 = (bf16[512,768]{1,0:T(8,128)(2,1)S(1)}, bf16[512,768]{1,0:T(8,128)(2,1)}, u32[]{:S(2)}) copy-start(bf16[512,768]{1,0:T(8,128)(2,1)} %reduce-scatter.9.cloned.1.call-done) | copy-start | bytes 2359300
  569.9 44.6 %copy-start.77 = (f32[512]{0:T(512)S(1)}, f32[512]{0:T(512)}, u32[]{:S(2)}) copy-start(f32[512]{0:T(512)} %copy-done.76) | copy-start | bytes 6148
  728.6 6.0 copy-start.64
  728.6 6.8 copy-start.51
  730.6 5.9 copy-start.50
  (57 other events, 106.3 us)
Sparse Core Ops, SparseCore 0:
  9.6 66.1 all-gather.4
  101.8 59.0 reduce-scatter.4
  165.4 63.3 all-gather.6
  241.9 59.0 reduce-scatter.6
  306.3 63.3 all-gather.8
  381.6 59.0 reduce-scatter.8
  446.6 63.3 all-gather.10
  550.9 60.1 reduce-scatter.10
  615.9 112.6 all-reduce.7
where the time goes:
time: 755 us; the launch traced here: 746 us
  waiting for transfers between devices  533 us (71%)
  matrix products  90 us (12%)
  blocking collectives  43.9 us (6%)
  other arithmetic  41.5 us (5%)
  local copies, waits for them, and re-layouts  20.5 us (3%)
  between operations  15.5 us (2%)
    psum x1, waiting for transfers between devices, body(): lax.psum((query_grad, key_grad, value_grad, output_grad, gate_grad, up_gr...  111 us
    all_gather x1, waiting for transfers between devices, body(): lax.all_gather(normed.astype(jnp.bfloat16), 'mp', axis=0, tiled=True)  63.5 us
    all_gather x1, waiting for transfers between devices, body(): lax.all_gather(d_resid_two.astype(jnp.bfloat16), 'mp', axis=0, tiled=True)  63.5 us
    all_gather x1, waiting for transfers between devices, body(): lax.all_gather(d_resid_one.astype(jnp.bfloat16), 'mp', axis=0, tiled=True)  63.2 us
    reduce_scatter x1, waiting for transfers between devices, body(): lax.psum_scatter((against(d_gate, gate_proj) + against(d_up, up_proj)).as...  59.2 us
    reduce_scatter x1, waiting for transfers between devices, body(): lax.psum_scatter(jnp.dot(mixed_low, out_proj, preferred_element_type=jnp....  59.1 us
    reduce_scatter x1, waiting for transfers between devices, body(): lax.psum_scatter(jnp.dot(hidden, down_proj, preferred_element_type=jnp.fl...  58.8 us
    all_gather x1, waiting for transfers between devices, body(): gathered = lax.all_gather(layer_in, 'mp', axis=0, tiled=True)  54.3 us
  transfers between devices with their start and end apart: 9, of which 8 were waited for; matrix products, arithmetic and copies ran while one was open for 5% of the time, Pallas kernels for 0%

commit v1 on v0

--- a/solution.py
+++ b/solution.py
@@ -5,6 +5,21 @@
 
 HS = 64
 SLOT_LEN = 1024
+
+
+def _attach_grid(xin, along_dim):
+    big = lax.axis_size("mp")
+    latest, block_next = (big, lax.axis_index("mp"))
+    local_now, t1 = (xin, 1)
+    while t1 < latest:
+        b_next = lax.ppermute(
+            local_now, axis_name="mp", perm=[(jj, jj ^ t1) for jj in range(latest)]
+        )
+        y1 = jnp.concatenate([local_now, b_next], axis=along_dim)
+        r1 = jnp.concatenate([b_next, local_now], axis=along_dim)
+        local_now = jnp.where(block_next & t1 == 0, y1, r1)
+        t1 = 2 * t1
+    return local_now
 
 
 def rms_norm(resid, gain):
@@ -213,7 +228,7 @@
     result, second_pull = jax.vjp(rms_norm, resid_two, second_gain)
     layer_out = result.astype(jnp.bfloat16)
     d_resid_two, second_part = second_pull(cotangent.astype(jnp.float32))
-    ffn_out_all = lax.all_gather(d_resid_two.astype(jnp.bfloat16), "mp", axis=0, tiled=True)
+    ffn_out_all = _attach_grid(d_resid_two.astype(jnp.bfloat16), along_dim=0)
     down_grad = cross(hidden, ffn_out_all)
     d_hidden = against(ffn_out_all, down_proj)
     unused, glu_pull = jax.vjp(swiglu, gate_pre, up_pre)

time: 755 us -> 789 us (1.045)
  waiting for transfers between devices: 533 us -> 556 us
    ppermute x0 -> x2, waiting for transfers between devices: none -> 85.8 us  [_attach_grid(): lax.ppermute(local_now, axis_name='mp', perm=[(jj, jj ^ t1) for jj in ran...]
    all_gather x1 -> x0, waiting for transfers between devices: 63.5 us -> none  [body(): lax.all_gather(d_resid_two.astype(jnp.bfloat16), 'mp', axis=0, tiled=True)]
  transfers between devices with their start and end apart: 9 -> 10, of which waited for: 8 -> 9; matrix products, arithmetic and copies ran while one was open for 5% -> 5% of each run, Pallas kernels for 0% -> 0%
where the time goes in v1:
time: 789 us; the launch traced here: 780 us
  waiting for transfers between devices  556 us (70%)
  matrix products  96.1 us (12%)
  other arithmetic  45.1 us (6%)
  blocking collectives  42 us (5%)
  local copies, waits for them, and re-layouts  20.7 us (3%)
  between operations  15.8 us (2%)
    psum x1, waiting for transfers between devices, body(): lax.psum((query_grad, key_grad, value_grad, output_grad, gate_grad, up_gr...  110 us
    ppermute x2, waiting for transfers between devices, _attach_grid(): lax.ppermute(local_now, axis_name='mp', perm=[(jj, jj ^ t1) for jj in ran...  85.8 us
    all_gather x1, waiting for transfers between devices, body(): lax.all_gather(normed.astype(jnp.bfloat16), 'mp', axis=0, tiled=True)  63.5 us
    all_gather x1, waiting for transfers between devices, body(): lax.all_gather(d_resid_one.astype(jnp.bfloat16), 'mp', axis=0, tiled=True)  63.3 us
    reduce_scatter x1, waiting for transfers between devices, body(): lax.psum_scatter((against(d_gate, gate_proj) + against(d_up, up_proj)).as...  60.6 us
    reduce_scatter x1, waiting for transfers between devices, body(): lax.psum_scatter(jnp.dot(mixed_low, out_proj, preferred_element_type=jnp....  59.1 us
    reduce_scatter x1, waiting for transfers between devices, body(): lax.psum_scatter(jnp.dot(hidden, down_proj, preferred_element_type=jnp.fl...  58.8 us
    all_gather x1, waiting for transfers between devices, body(): gathered = lax.all_gather(layer_in, 'mp', axis=0, tiled=True)  54.3 us
  transfers between devices with their start and end apart: 10, of which 9 were waited for; matrix products, arithmetic and copies ran while one was open for 5% of the time, Pallas kernels for 0%

profile of v1, /device:TPU:0, one launch (start us, length us, event | category | flops | bytes accessed | tf_op | source)
XLA Modules:
  0.0 780.0 jit_solution(4919859925644502734)
XLA Ops:
  19.7 1.8 multiply_cosine_fusion
  21.5 54.3 %all-gather.4.cloned.1.call-done = bf16[2048,768]{1,0:T(8,128)(2,1)} async-done(((bf16[512,768]{1,0:T(8,128)(2,1)}), bf16[2048,768]{1,0:T(8,128)(2,1)}) %all-gather.4.cloned.1.call-update) | async-done | bytes 3145744 | tf_op jit(solution)/shard_map/all_gather | solution.py:189
  75.8 3.2 convolution_convert_fusion.3
  88.0 3.7 exponential_reduce_fusion
  93.9 2.0 fusion.38
  95.9 2.0 fusion.36
  98.9 2.8 convolution_convert_fusion.1
  101.8 59.1 %reduce-scatter.5.cloned.1.call-done = bf16[512,768]{1,0:T(8,128)(2,1)} async-done(((bf16[2048,768]{1,0:T(8,128)(2,1)}), bf16[512,768]{1,0:T(8,128)(2,1)}) %reduce-scatter.5.cloned.1.call-update) | async-done | bytes 786448 | tf_op jit(solution)/shard_map/reduce_scatter | solution.py:209
  163.0 2.3 multiply_convert_fusion.7
  165.4 63.5 %all-gather.6.cloned.1.call-done = bf16[2048,768]{1,0:T(8,128)(2,1)} async-done(((bf16[512,768]{1,0:T(8,128)(2,1)}), bf16[2048,768]{1,0:T(8,128)(2,1)}) %all-gather.6.cloned.1.call-update) | async-done | bytes 3145744 | tf_op jit(solution)/shard_map/all_gather | solution.py:217
  228.8 3.8 fusion.123
  232.7 4.3 multiply_convert_fusion.3
  238.4 3.5 convolution_convert_fusion
  242.4 58.8 %reduce-scatter.7.cloned.1.call-done = bf16[512,768]{1,0:T(8,128)(2,1)} async-done(((bf16[2048,768]{1,0:T(8,128)(2,1)}), bf16[512,768]{1,0:T(8,128)(2,1)}) %reduce-scatter.7.cloned.1.call-update) | async-done | bytes 786448 | tf_op jit(solution)/shard_map/reduce_scatter | solution.py:221
  301.1 1.8 multiply_reduce_fusion.6
  304.1 2.2 fusion.116
  307.2 18.3 %collective-permute-done = bf16[512,768]{1,0:T(8,128)(2,1)} collective-permute-done((bf16[512,768]{1,0:T(8,128)(2,1)}, bf16[512,768]{1,0:T(8,128)(2,1)}, u32[]{:S(2)}, u32[]{:S(2)}) %collective-permute-start) | collective-permute-done | bytes 786464 | tf_op jit(solution)/shard_map/ppermute | solution.py:15
  325.5 3.6 maximum_select_fusion.1
  329.1 2.7 collective-permute-start.1
  331.8 67.5 %collective-permute-done.1 = bf16[1024,768]{1,0:T(8,128)(2,1)} collective-permute-done((bf16[1024,768]{1,0:T(8,128)(2,1)}, bf16[1024,768]{1,0:T(8,128)(2,1)}, u32[]{:S(2)}, u32[]{:S(2)}) %collective-permute-start.1) | collective-permute-done | bytes 1572896 | tf_op jit(solution)/shard_map/ppermute | solution.py:15
  399.3 9.0 %multiply_convert_fusion.2 = (bf16[2048,512]{1,0:T(8,128)(2,1)S(1)}, bf16[2048,512]{1,0:T(8,128)(2,1)S(1)}) fusion(f32[2048,512]{1,0:T(8,128)} %copy-done.89, f32[2048,512]{1,0:T(8,128)} %get-tuple-element.194, bf16[512,768]{1,0:T(8,128)(2,1)S(1)} %copy-done, bf16[1024,768]{1,0:T(8,128)(2,1)} %collective-permute-done.1, ...), kind=kOutput, calls=%fused_computation.18 | convolution fusion | flops 1639448576 | bytes 16515073 | tf_op jit(solution)/shard_map/dot_general | solution.py:66
  408.3 1.9 fusion.124
  410.4 3.6 add_convert_fusion.1
  414.0 60.6 %reduce-scatter.9.cloned.1.call-done = bf16[512,768]{1,0:T(8,128)(2,1)} async-done(((bf16[2048,768]{1,0:T(8,128)(2,1)}), bf16[512,768]{1,0:T(8,128)(2,1)}) %reduce-scatter.9.cloned.1.call-update) | async-done | bytes 786448 | tf_op jit(solution)/shard_map/reduce_scatter | solution.py:240
  474.6 3.0 multiply_reduce_fusion.4
  480.7 63.3 %all-gather.8.cloned.1.call-done = bf16[2048,768]{1,0:T(8,128)(2,1)} async-done(((bf16[512,768]{1,0:T(8,128)(2,1)}), bf16[2048,768]{1,0:T(8,128)(2,1)}) %all-gather.8.cloned.1.call-update) | async-done | bytes 3145744 | tf_op jit(solution)/shard_map/all_gather | solution.py:247
  543.9 3.1 convolution_convert_fusion.2
  547.1 3.0 convolution_bitcast_fusion.5
  558.7 2.5 multiply_reduce_fusion.1
  561.2 2.6 fusion.25
  563.9 2.7 multiply_reduce_fusion
  566.6 2.6 fusion.24
  569.2 1.8 multiply_convert_fusion
  572.8 1.8 multiply_convert_fusion.1
  581.9 2.8 add_convert_fusion
  585.0 5.7 fusion.129
  590.8 3.0 fusion.128
  593.8 6.2 fusion.43
  599.9 1.6 fusion.127
  602.3 1.6 convolution_bitcast_fusion.2
  603.9 1.6 convolution_bitcast_fusion.3
  605.4 1.6 convolution_bitcast_fusion.4
  607.8 42.0 %all-reduce.4 = (f32[768]{0:T(1024)}, f32[768]{0:T(1024)}) all-reduce(f32[768]{0:T(1024)S(1)} %copy-done.79, f32[768]{0:T(1024)S(1)} %copy-done.78), channel_id=1, replica_groups=mesh['dp'=8,'mp'=4] {'dp','mp'}, use_global_device_ids=true, to_apply=%region_28.29 | all-reduce | flops 1536 | bytes 12288 | tf_op jit(solution)/shard_map/psum | solution.py:277
  649.7 3.2 add_convert_fusion.2
  652.9 109.5 %all-reduce.8.cloned.1.call-done = (f32[768,192]{0,1:T(8,128)}, f32[768,192]{0,1:T(8,128)}, f32[768,192]{0,1:T(8,128)}, f32[192,768]{1,0:T(8,128)}, f32[768,512]...) async-done(((f32[768,192]{0,1:T(8,128)}, f32[768,192]{0,1:T(8,128)}, f32[768,192]{0,1:T(8,128)}, f32[192,768]{1,0:T(8,128)}, f32[768,512]{1,0:T(8,128)}, ...) | async-done | bytes 7077904 | tf_op jit(solution)/shard_map/psum | solution.py:274
  762.4 2.1 copy.46
  764.5 2.0 copy.47
  766.5 1.9 copy.48
  (278 shorter events, 56.9 us)
Async XLA Ops:
  7.2 231.2 %copy-start = (bf16[512,768]{1,0:T(8,128)(2,1)S(1)}, bf16[512,768]{1,0:T(8,128)(2,1)}, u32[]{:S(2)}) copy-start(bf16[512,768]{1,0:T(8,128)(2,1)} %param.43) | copy-start | bytes 2359300
  7.2 68.6 %all-gather.4.cloned.1.call-start = ((), (), s32[]{:S(2)}) async-start(), calls=%async_computation.4 | async-start | bytes 3932160 | tf_op jit(solution)/shard_map/all_gather | solution.py:189
  7.9 153.0 %reduce-scatter.5.cloned.1.call-start = ((), (), s32[]{:S(2)}) async-start(), calls=%async_computation.5 | async-start | bytes 3932160 | tf_op jit(solution)/shard_map/reduce_scatter | solution.py:209
  18.1 74.7 %copy-start.34 = (pred[512,512]{0,1:T(8,128)(4,1)}, pred[512,512]{0,1:T(8,128)(4,1)S(1)}, u32[]{:S(2)}) copy-start(pred[512,512]{0,1:T(8,128)(4,1)S(1)} %fusion.40) | copy-start | bytes 786436
  18.3 73.5 %copy-start.32 = (pred[512,512]{0,1:T(8,128)(4,1)}, pred[512,512]{0,1:T(8,128)(4,1)S(1)}, u32[]{:S(2)}) copy-start(pred[512,512]{0,1:T(8,128)(4,1)S(1)} %fusion.41) | copy-start | bytes 786436
  19.7 76.2 %copy-start.15 = (pred[512,1024]{1,0:T(8,128)(4,1)}, pred[512,1024]{1,0:T(8,128)(4,1)S(1)}, u32[]{:S(2)}) copy-start(pred[512,1024]{1,0:T(8,128)(4,1)S(1)} %get-tuple-element.182) | copy-start | bytes 1572868
  21.5 57.6 %copy-start.53 = (bf16[768,192]{0,1:T(8,128)(2,1)S(1)}, bf16[768,192]{0,1:T(8,128)(2,1)}, u32[]{:S(2)}) copy-start(bf16[768,192]{0,1:T(8,128)(2,1)} %param.38) | copy-start | bytes 884740
  79.0 12.7 %copy-start.55 = (bf16[512,192]{0,1:T(8,128)(2,1)}, bf16[512,192]{0,1:T(8,128)(2,1)S(1)}, u32[]{:S(2)}) copy-start(bf16[512,192]{0,1:T(8,128)(2,1)S(1)} %get-tuple-element.171) | copy-start | bytes 589828
  79.0 13.8 %copy-start.57 = (bf16[512,192]{0,1:T(8,128)(2,1)}, bf16[512,192]{0,1:T(8,128)(2,1)S(1)}, u32[]{:S(2)}) copy-start(bf16[512,192]{0,1:T(8,128)(2,1)S(1)} %get-tuple-element.172) | copy-start | bytes 589828
  79.1 14.7 %copy-start.46 = (bf16[1024,192]{0,1:T(8,128)(2,1)}, bf16[1024,192]{0,1:T(8,128)(2,1)S(1)}, u32[]{:S(2)}) copy-start(bf16[1024,192]{0,1:T(8,128)(2,1)S(1)} %get-tuple-element.173) | copy-start | bytes 1179652
  79.1 16.7 %copy-start.44 = (bf16[1024,192]{0,1:T(8,128)(2,1)}, bf16[1024,192]{0,1:T(8,128)(2,1)S(1)}, u32[]{:S(2)}) copy-start(bf16[1024,192]{0,1:T(8,128)(2,1)S(1)} %get-tuple-element.174) | copy-start | bytes 1179652
  82.1 4.5 copy-start.42
  82.9 8.9 %copy-start.6 = (f32[3,512,512]{1,2,0:T(8,128)}, f32[3,512,512]{1,2,0:T(8,128)S(1)}, u32[]{:S(2)}) copy-start(f32[3,512,512]{1,2,0:T(8,128)S(1)} %get-tuple-element.192) | copy-start | bytes 9437188
  83.6 8.2 %copy-start.71 = (f32[3,512]{1,0:T(4,128)}, f32[3,512]{1,0:T(4,128)S(1)}, u32[]{:S(2)}) copy-start(f32[3,512]{1,0:T(4,128)S(1)} %log_add_fusion.3) | copy-start | bytes 18436
  84.4 8.4 %copy-start.8 = (f32[3,512,512]{1,2,0:T(8,128)}, f32[3,512,512]{1,2,0:T(8,128)S(1)}, u32[]{:S(2)}) copy-start(f32[3,512,512]{1,2,0:T(8,128)S(1)} %get-tuple-element.188) | copy-start | bytes 9437188
  85.1 7.7 copy-start.73
  86.6 7.3 copy-start.5
  87.9 7.9 %copy-start.4 = (f32[3,512,1024]{2,1,0:T(8,128)}, f32[3,512,1024]{2,1,0:T(8,128)S(1)}, u32[]{:S(2)}) copy-start(f32[3,512,1024]{2,1,0:T(8,128)S(1)} %get-tuple-element.186) | copy-start | bytes 18874372
  101.7 59.2 %copy-start.10 = (bf16[512,768]{1,0:T(8,128)(2,1)S(1)}, bf16[512,768]{1,0:T(8,128)(2,1)}, u32[]{:S(2)}) copy-start(bf16[512,768]{1,0:T(8,128)(2,1)} %param.36) | copy-start | bytes 2359300
  101.7 61.3 %copy-start.68 = (f32[768]{0:T(1024)S(1)}, f32[768]{0:T(1024)}, u32[]{:S(2)}) copy-start(f32[768]{0:T(1024)} %param.44) | copy-start | bytes 9220
  101.7 127.1 %copy-start.59 = (bf16[768,512]{1,0:T(8,128)(2,1)S(1)}, bf16[768,512]{1,0:T(8,128)(2,1)}, u32[]{:S(2)}) copy-start(bf16[768,512]{1,0:T(8,128)(2,1)} %param.41) | copy-start | bytes 2359300
  101.7 127.1 %all-gather.6.cloned.1.call-start = ((), (), s32[]{:S(2)}) async-start(), calls=%async_computation.6 | async-start | bytes 3932160 | tf_op jit(solution)/shard_map/all_gather | solution.py:217
  165.3 135.8 %reduce-scatter.7.cloned.1.call-start = ((), (), s32[]{:S(2)}) async-start(), calls=%async_computation.7 | async-start | bytes 3932160 | tf_op jit(solution)/shard_map/reduce_scatter | solution.py:221
  232.7 4.4 copy-start.89
  241.9 59.2 %copy-start.11 = (bf16[512,768]{1,0:T(8,128)(2,1)S(1)}, bf16[512,768]{1,0:T(8,128)(2,1)}, u32[]{:S(2)}) copy-start(bf16[512,768]{1,0:T(8,128)(2,1)} %reduce-scatter.5.cloned.1.call-done) | copy-start | bytes 2359300
  241.9 232.7 %reduce-scatter.9.cloned.1.call-start = ((), (), s32[]{:S(2)}) async-start(), calls=%async_computation.8 | async-start | bytes 3932160 | tf_op jit(solution)/shard_map/reduce_scatter | solution.py:240
  306.3 19.2 %collective-permute-start = (bf16[512,768]{1,0:T(8,128)(2,1)}, bf16[512,768]{1,0:T(8,128)(2,1)}, u32[]{:S(2)}, u32[]{:S(2)}) collective-permute-start(bf16[512,768]{1,0:T(8,128)(2,1)} %get-tuple-element.152), channel_id=1, source_target_pairs={{0,1},{1,0},{2,3},{3,2},{4,5},{5,4},{6,7},{7,6},{8,9},{9,8},{10,11... | collective-permute-start | bytes 2359304 | tf_op jit(solution)/shard_map/ppermute | solution.py:15
  329.1 70.2 %collective-permute-start.1 = (bf16[1024,768]{1,0:T(8,128)(2,1)}, bf16[1024,768]{1,0:T(8,128)(2,1)}, u32[]{:S(2)}, u32[]{:S(2)}) collective-permute-start(bf16[1024,768]{1,0:T(8,128)(2,1)} %maximum_select_fusion.1), channel_id=1, source_target_pairs={{0,2},{1,3},{2,0},{3,1},{4,6},{5,7},{6,4},{7,5},{8,10},{9,11},{10,... | collective-permute-start | bytes 4718600 | tf_op jit(solution)/shard_map/ppermute | solution.py:15
  399.3 9.0 %copy-start.60 = (bf16[768,512]{1,0:T(8,128)(2,1)S(1)}, bf16[768,512]{1,0:T(8,128)(2,1)}, u32[]{:S(2)}) copy-start(bf16[768,512]{1,0:T(8,128)(2,1)} %param.41) | copy-start | bytes 2359300
  414.0 130.0 %all-gather.8.cloned.1.call-start = ((), (), s32[]{:S(2)}) async-start(), calls=%async_computation.9 | async-start | bytes 3932160 | tf_op jit(solution)/shard_map/all_gather | solution.py:247
  474.6 4.3 copy-start.12
  474.6 4.3 copy-start.30
  480.4 66.7 %copy-start.35 = (pred[512,512]{0,1:T(8,128)(4,1)S(1)}, pred[512,512]{0,1:T(8,128)(4,1)}, u32[]{:S(2)}) copy-start(pred[512,512]{0,1:T(8,128)(4,1)} %copy-done.34) | copy-start | bytes 786436
  480.4 66.7 %copy-start.74 = (f32[3,512]{1,0:T(4,128)S(1)}, f32[3,512]{1,0:T(4,128)}, u32[]{:S(2)}) copy-start(f32[3,512]{1,0:T(4,128)} %copy-done.73) | copy-start | bytes 18436
  480.4 66.7 %copy-start.82 = (bf16[512]{0:T(512)(128)(2,1)S(1)}, bf16[512]{0:T(512)(128)(2,1)}, u32[]{:S(2)}) copy-start(bf16[512]{0:T(512)(128)(2,1)} %get-tuple-element.206) | copy-start | bytes 3076
  480.5 169.3 %reduce-scatter.11.cloned.1.call-start = ((), (), s32[]{:S(2)}) async-start(), calls=%async_computation.10 | async-start | bytes 3932160 | tf_op jit(solution)/shard_map/reduce_scatter | solution.py:263
  558.0 5.8 slice-start
  558.7 5.2 slice-start.1
  584.7 177.7 %all-reduce.8.cloned.1.call-start = ((), (), s32[]{:S(2)}) async-start(), calls=%async_computation.11 | async-start | bytes 14155776 | tf_op jit(solution)/shard_map/psum | solution.py:274
  585.0 5.8 copy-start.18
  585.0 5.8 copy-start.20
  593.8 6.2 copy-start.22
  593.8 6.2 copy-start.36
  607.1 42.7 %copy-start.31 = (bf16[512,768]{1,0:T(8,128)(2,1)S(1)}, bf16[512,768]{1,0:T(8,128)(2,1)}, u32[]{:S(2)}) copy-start(bf16[512,768]{1,0:T(8,128)(2,1)} %reduce-scatter.9.cloned.1.call-done) | copy-start | bytes 2359300
  607.1 42.7 %copy-start.76 = (f32[512]{0:T(512)S(1)}, f32[512]{0:T(512)}, u32[]{:S(2)}) copy-start(f32[512]{0:T(512)} %copy-done.75) | copy-start | bytes 6148
  762.4 6.0 copy-start.63
  762.4 6.8 copy-start.50
  764.5 5.9 copy-start.49
  (58 other events, 112.6 us)
Sparse Core Ops, SparseCore 0:
  9.6 66.1 all-gather.3
  101.8 59.0 reduce-scatter.4
  165.4 63.3 all-gather.5
  242.0 59.0 reduce-scatter.6
  414.1 60.4 reduce-scatter.8
  480.5 63.3 all-gather.7
  584.8 59.9 reduce-scatter.10
  649.7 112.7 all-reduce.7
